TPU v7x, 32 devices: a whole 2x2x4 slice. The times are simulated.
32 devices in a mesh: groups: 1, ctx: 32 (over z, y, x, core).
Axes of the slice: x: 2, y: 2, z: 4, core: 2. Of those that a mesh axis runs over, the one named last changes fastest.
Arguments:
- prefill_query: bfloat16 [1024, 32, 576], P('groups', 'ctx'), may hold values from -1000 to 1000
- prefill_latent: bfloat16 [1024, 576], P(('groups', 'ctx')), may hold values from -6 to 6
- decode_query: bfloat16 [2, 32, 576], P('groups'), may hold values from -1000 to 1000
- cache: bfloat16 [2, 16384, 576], P('groups', 'ctx'), may hold values from -6 to 6
- lengths: int32 [2], P('groups'), may hold values from 2049 to 16384
- page_table: int32 [64, 2], P('groups'), may hold values from 0 to 31, as said below
Outputs:
- prefill_out: bfloat16 [1024, 32, 512], P('groups', 'ctx')
- decode_out: bfloat16 [2, 32, 512], P('groups', 'ctx')
Inputs may be any that keep to these rules, and one draw needn't show every extreme that they name: `page_table`: row p names the device (column 0, below 32) and the pool slot (column 1, below 16) that take latent page p; no two rows name the same pair.
All inputs are finite; a program needn't handle non-finite values.
Results may differ from a plain program's by a relative error of at most 0.0049.
Values may be sent and summed in bfloat16 or wider, within the bound.
A program may use at most 64 MiB of HBM per device.

v0:
```python
import functools

import jax
import jax.numpy as jnp
from jax import lax
from jax.experimental import pallas as pl
from jax.experimental.pallas import tpu as pltpu
from jax.sharding import PartitionSpec as P

D_LAT = 512
PAGE = 16
POOL = 16
REQ = 2

SCALE = 192.0 ** (-0.5)
NEG = -1e30
MSG = D_LAT + 128


def kernel(
    n,
    qt_hbm,
    lat_hbm,
    dq_hbm,
    ct_hbm,
    len_ref,
    pt_ref,
    pout_ref,
    dout_ref,
    held,
    dq_ref,
    qt,
    q,
    ct,
    parts,
    mate,
    joined,
    moved,
    local_sem,
    z_sem,
    x_sem,
    y_sem,
    pair_sem,
    dx_sem,
    dy_sem,
    full_sem,
    half_sem,
    dsend_sem,
    drecv_sem,
    ready_sem,
    mate_sem,
):
    me = lax.axis_index("ctx")
    line = n // 8
    core = me % 2
    x = (me // 2) % 2
    y = (me // 4) % 2
    z = me // 8
    rows = lat_hbm.shape[0]
    heads = dq_ref.shape[1]
    chips = n // 2
    span = qt.shape[1]
    cache_dev = ct.shape[2]

    def opposite(step):
        result, bit = z, 1
        while bit <= step:
            if step // bit % 2:
                result = result + bit * (1 - 2 * (z // bit % 2))
            bit *= 2
        return result

    lines = [opposite(step) for step in range(line)]

    def block(step, by, bx, bc):
        return ((lines[step] * 2 + by) * 2 + bx) * 2 + bc

    x_peer = block(0, y, 1 - x, core)
    y_peer = block(0, 1 - y, x, core)
    pair = block(0, y, x, 1 - core)

    own_copy = pltpu.make_async_copy(lat_hbm, held.at[me], local_sem.at[0])
    own_copy.start()
    q_copy = pltpu.make_async_copy(qt_hbm, qt, local_sem.at[1])
    q_copy.start()
    c_copy = pltpu.make_async_copy(ct_hbm, ct, local_sem.at[2])
    c_copy.start()
    d_copy = pltpu.make_async_copy(dq_hbm, dq_ref, local_sem.at[3])
    d_copy.start()

    barrier = pltpu.get_barrier_semaphore()

    near = [x_peer, y_peer, pair] + [block(step, y, x, core) for step in range(1, line)]
    for target in near:
        pl.semaphore_signal(barrier, inc=1, device_id={"ctx": target})

    split = rows // 2 if rows % 32 == 0 else rows

    def move(index, send, recv, target, part=None):
        ref = held.at[index]
        if part == 0:
            ref = held.at[index, pl.ds(0, split)]
        if part == 1:
            ref = held.at[index, pl.ds(split, rows - split)]
        return pltpu.make_async_remote_copy(
            src_ref=ref, dst_ref=ref, send_sem=send, recv_sem=recv, device_id={"ctx": target}
        )

    sends = []

    def go(copy):
        copy.start()
        sends.append(copy)

    def to_pair(step, by, bx):
        index = block(step, by, bx, core)
        spot = (step * 2 + (0 if by is y else 1)) * 2 + (0 if bx is x else 1)
        go(move(index, pair_sem.at[spot], full_sem.at[index], pair))

    def full_wait(index):
        move(index, z_sem.at[0], full_sem.at[index], pair).wait_recv()

    def half_wait(index):
        move(index, z_sem.at[0], half_sem.at[index, 0], pair, 0).wait_recv()
        if split < rows:
            move(index, z_sem.at[0], half_sem.at[index, 1], pair, 1).wait_recv()

    far_x, far_y = 1 - x, 1 - y

    def spread_column(step):
        index = block(step, y, x, core)
        go(move(index, x_sem.at[step], full_sem.at[index], x_peer))
        go(move(index, y_sem.at[step], full_sem.at[index], y_peer))
        to_pair(step, y, x)

    def spread_plane(step):
        index = block(step, y, far_x, core)
        full_wait(index)
        if split < rows:
            go(move(index, dy_sem.at[step], half_sem.at[index, 1], y_peer, 1))
        to_pair(step, y, far_x)
        index = block(step, far_y, x, core)
        full_wait(index)
        go(move(index, dx_sem.at[step], half_sem.at[index, 0], x_peer, 0))
        to_pair(step, far_y, x)

    q_copy.wait()
    for start in range(0, span, 128):
        q[start : start + 128, :] = qt[:, start : start + 128].T
    own_copy.wait()
    pl.semaphore_wait(barrier, len(near))

    pl.semaphore_signal(ready_sem.at[0], inc=1, device_id={"ctx": x_peer})
    spread_column(0)
    for step in range(1, line):
        go(move(me, z_sem.at[step], full_sem.at[me], block(step, y, x, core)))
    c_copy.wait()
    d_copy.wait()
    latent = held[me]
    row_page = (me * rows + lax.broadcasted_iota(jnp.int32, (1, rows), 1)) // PAGE
    first_page = me * rows // PAGE
    request_of = jnp.zeros((1, rows), jnp.int32)
    for p in range(max(1, rows // PAGE)):
        page = first_page + p
        request = (pt_ref[0, page] * POOL + pt_ref[1, page]) % REQ
        request_of = jnp.where(row_page == page, request, request_of)
    positions = me * cache_dev + lax.broadcasted_iota(jnp.int32, (1, cache_dev), 1)
    nt = (((1,), (1,)), ((), ()))
    for r in range(REQ):
        queries = dq_ref[r]
        keys = ct[r]
        scores = jnp.dot(queries, keys, preferred_element_type=jnp.float32) * SCALE
        page_scores = (
            lax.dot_general(queries, latent, nt, preferred_element_type=jnp.float32) * SCALE
        )
        ok = positions < len_ref[r]
        page_ok = request_of == r
        scores = jnp.where(ok, scores, NEG)
        page_scores = jnp.where(page_ok, page_scores, NEG)
        top = jnp.maximum(
            jnp.max(scores, axis=1, keepdims=True), jnp.max(page_scores, axis=1, keepdims=True)
        )
        weights = jnp.where(ok, jnp.exp(scores - top), 0.0)
        page_weights = jnp.where(page_ok, jnp.exp(page_scores - top), 0.0)
        total = jnp.sum(weights, axis=1, keepdims=True) + jnp.sum(
            page_weights, axis=1, keepdims=True
        )
        mixed = lax.dot_general(
            weights.astype(jnp.bfloat16), keys[:D_LAT], nt, preferred_element_type=jnp.float32
        ) + jnp.dot(
            page_weights.astype(jnp.bfloat16),
            latent[:, :D_LAT],
            preferred_element_type=jnp.float32,
        )
        lane = lax.broadcasted_iota(jnp.int32, (heads, 128), 1)
        tail = jnp.where(lane < 64, top, total)
        parts[:, :, :, r * MSG : r * MSG + D_LAT] = mixed.reshape(chips, 2, 1, D_LAT)
        parts[:, :, :, r * MSG + D_LAT : (r + 1) * MSG] = tail.reshape(chips, 2, 1, 128)

    mate_copy = pltpu.make_async_remote_copy(
        src_ref=parts.at[:, 1 - core],
        dst_ref=mate,
        send_sem=mate_sem.at[0],
        recv_sem=mate_sem.at[1],
        device_id={"ctx": pair},
    )
    mate_copy.start()

    def part_copy(target, source):
        return pltpu.make_async_remote_copy(
            src_ref=joined.at[target],
            dst_ref=moved.at[source],
            send_sem=dsend_sem.at[target],
            recv_sem=drecv_sem.at[source],
            device_id={"ctx": target * 2 + core},
        )

    chip = me // 2

    def ready(stage, target):
        pl.semaphore_signal(ready_sem.at[stage], inc=1, device_id={"ctx": target})

    def send_part(step, carry):
        part_copy((chip + step) % chips, chip).start()
        return carry

    def join():
        mate_copy.wait_recv()
        for r in range(REQ):
            mine = parts[:, core, :, r * MSG : (r + 1) * MSG].reshape(chips, MSG)
            other = mate[:, :, r * MSG : (r + 1) * MSG].reshape(chips, MSG)
            top_mine = mine[:, D_LAT : D_LAT + 1]
            top_other = other[:, D_LAT : D_LAT + 1]
            top = jnp.maximum(top_mine, top_other)
            both = mine * jnp.exp(top_mine - top) + other * jnp.exp(top_other - top)
            lane = lax.broadcasted_iota(jnp.int32, (chips, 128), 1)
            tail = jnp.where(lane < 64, top, both[:, D_LAT:])
            joined[:, :, r * MSG : r * MSG + D_LAT] = both[:, :D_LAT].reshape(chips, 1, D_LAT)
            joined[:, :, r * MSG + D_LAT : (r + 1) * MSG] = tail.reshape(chips, 1, 128)
        moved[chip] = joined[chip]

    pl.semaphore_wait(ready_sem.at[0], 1)
    ready(1, y_peer)
    spread_plane(0)
    join()
    pl.semaphore_wait(ready_sem.at[1], 1)
    lax.fori_loop(1, chips, send_part, 0)
    for step in range(1, line):
        full_wait(block(step, y, x, core))
        spread_column(step)
    for step in range(1, line):
        spread_plane(step)
    for step in range(line):
        index = block(step, far_y, far_x, core)
        half_wait(index)
        to_pair(step, far_y, far_x)
    for step in range(line):
        for by in (y, far_y):
            for bx in (x, far_x):
                index = block(step, by, bx, 1 - core)
                full_wait(index)

    chunk = min(256, span)
    for start in range(0, span, chunk):
        stop = start + chunk
        keys = held[: stop // rows].reshape(stop, held.shape[2])
        scores = lax.dot_general(
            q[start:stop], keys, nt, preferred_element_type=jnp.float32
        )
        row = start + lax.broadcasted_iota(jnp.int32, (chunk, stop), 0)
        col = lax.broadcasted_iota(jnp.int32, (chunk, stop), 1)
        scores = jnp.where(col <= row, scores, NEG)
        top = jnp.max(scores, axis=1, keepdims=True)
        weights = jnp.exp((scores - top) * SCALE)
        total = jnp.sum(weights, axis=1, keepdims=True)
        mixed = jnp.dot(
            weights.astype(jnp.bfloat16), keys[:, :D_LAT], preferred_element_type=jnp.float32
        )
        pout_ref[start:stop, :] = (mixed / total).astype(jnp.bfloat16)

    def await_part(step, carry):
        source = (chip + step) % chips
        part_copy(source, source).wait_recv()
        return carry

    lax.fori_loop(1, chips, await_part, 0)
    for r in range(REQ):
        piece = moved[:, :, r * MSG : (r + 1) * MSG].reshape(chips, MSG)
        tops = piece[:, D_LAT : D_LAT + 1]
        sums = piece[:, D_LAT + 64 : D_LAT + 65]
        factor = jnp.exp(tops - jnp.max(tops, axis=0, keepdims=True))
        own_sum = jnp.sum(sums * factor, axis=0, keepdims=True)
        own_out = jnp.sum(piece[:, :D_LAT] * factor, axis=0, keepdims=True)
        dout_ref[r : r + 1, :] = (own_out / own_sum).astype(jnp.bfloat16)

    for copy in sends:
        copy.wait_send()

    def drain(step, carry):
        part_copy((chip + step) % chips, chip).wait_send()
        return carry

    mate_copy.wait_send()
    lax.fori_loop(1, chips, drain, 0)


def shards(n, prefill_query, prefill_latent, decode_query, cache, lengths, page_table):
    span, head_here, width = prefill_query.shape
    rows = prefill_latent.shape[0]
    heads = decode_query.shape[1]
    cache_dev = cache.shape[1]
    if head_here != 1 or n % 8 or rows * n != span:
        raise ValueError("unexpected sizes")
    line = n // 8
    vmem = pl.BlockSpec(memory_space=pltpu.VMEM)
    smem = pl.BlockSpec(memory_space=pltpu.SMEM)
    anywhere = pl.BlockSpec(memory_space=pl.ANY)
    dma = pltpu.SemaphoreType.DMA
    prefill_out, decode_out = pl.pallas_call(
        functools.partial(kernel, n),
        out_shape=(
            pltpu.VMEM((span, D_LAT), jnp.bfloat16),
            pltpu.VMEM((REQ, D_LAT), jnp.bfloat16),
        ),
        in_specs=[anywhere, anywhere, anywhere, anywhere, smem, smem],
        out_specs=(vmem, vmem),
        scratch_shapes=[
            pltpu.VMEM((n, rows, width), jnp.bfloat16),
            pltpu.VMEM((REQ, heads, width), jnp.bfloat16),
            pltpu.VMEM((width, span), jnp.bfloat16),
            pltpu.VMEM((span, width), jnp.bfloat16),
            pltpu.VMEM((REQ, width, cache_dev), jnp.bfloat16),
            pltpu.VMEM((n // 2, 2, 1, REQ * MSG), jnp.float32),
            pltpu.VMEM((n // 2, 1, REQ * MSG), jnp.float32),
            pltpu.VMEM((n // 2, 1, REQ * MSG), jnp.float32),
            pltpu.VMEM((n // 2, 1, REQ * MSG), jnp.float32),

            dma((4,)),
            dma((line,)),
            dma((line,)),
            dma((line,)),
            dma((line * 4,)),
            dma((line,)),
            dma((line,)),
            dma((n,)),
            dma((n, 2)),
            dma((n // 2,)),
            dma((n // 2,)),
            pltpu.SemaphoreType.REGULAR((2,)),
            dma((2,)),
        ],
        compiler_params=pltpu.CompilerParams(collective_id=0, has_side_effects=True),
    )(
        prefill_query[:, 0, :].T,
        prefill_latent,
        decode_query,
        jnp.swapaxes(cache, 1, 2),
        lengths,
        page_table.T,
    )
    return prefill_out[:, None, :], decode_out[:, None, :]


def solution(mesh):
    in_specs = (
        P("groups", "ctx", None),
        P(("groups", "ctx"), None),
        P("groups", None, None),
        P("groups", "ctx", None),
        P("groups"),
        P("groups", None),
    )
    out_specs = (P("groups", "ctx", None), P("groups", "ctx", None))
    return jax.shard_map(
        functools.partial(shards, mesh.shape["ctx"]),
        mesh=mesh,
        in_specs=in_specs,
        out_specs=out_specs,
        check_vma=False,
    )
```

profile of v0, /device:TPU:1, one launch (start us, length us, event | category | flops | bytes accessed | tf_op | source)
XLA Modules:
  0.0 26.3 jit_solution(13020431505055458695)
XLA Ops:
  0.6 24.1 %shard_map.77 = (bf16[1024,512]{1,0:T(8,128)(2,1)S(1)}, bf16[2,512]{1,0:T(2,128)(2,1)S(1)}) custom-call(bf16[576,1024]{1,0:T(8,128)(2,1)} %bitcast.9, bf16[32,576]{1,0:T(8,128)(2,1)} %lat_hbm.1, bf16[2,32,576]{2,1,0:T(8,128)(2,1)} %dq_hbm.1, bf16[2,576,512]{2,1,0:T(8,128)(2,1)} %bitcast.10, s32[2]{0:T(128)} %len_ref.1, s32[2,64]{1,0:T(2,128)} %bitcast.11), custom_call_target="tpu_custom_call" | custom-call | tf_op jit(solution)/shard_map/pallas_call | solution.py:319
  24.7 1.0 %copy.10 = bf16[1024,1,512]{2,0,1:T(8,128)(2,1)} copy(bf16[1024,1,512]{2,0,1:T(8,128)(2,1)S(1)} %bitcast.7) | data formatting | bytes 2097152
  25.7 0.6 %copy.11 = bf16[2,1,512]{2,0,1:T(2,128)(2,1)} copy(bf16[2,1,512]{2,0,1:T(2,128)(2,1)S(1)} %bitcast.8) | data formatting | bytes 4096
where the time goes:
time: 26.4 us; the launch traced here: 26.3 us
  Pallas kernels  24.1 us (91%)
  local copies, waits for them, and re-layouts  1.55 us (6%)
  between operations  0.64 us (2%)
    pallas_call x1, Pallas kernels, shards(): pl.pallas_call(functools.partial(kernel, n), out_shape=(pltpu.VMEM((span,...  24.1 us
    unnamed x2, local copies, waits for them, and re-layouts  1.55 us

commit v1 on v0

v1 whole, which is shorter than its diff:
```python
import functools

import jax
import jax.numpy as jnp
from jax import lax
from jax.experimental import pallas as pl
from jax.experimental.pallas import tpu as pltpu
from jax.sharding import PartitionSpec as P

D_LAT = 512
PAGE = 16
POOL = 16
REQ = 2

SCALE = 192.0 ** (-0.5)
NEG = -1e30
MSG = D_LAT + 128
NT = (((1,), (1,)), ((), ()))


def kernel(
    n,
    qt_hbm,
    lat_hbm,
    dq_hbm,
    ct_hbm,
    len_hbm,
    pt_hbm,
    pout_ref,
    dout_ref,
    held,
    dq_ref,
    qt,
    q,
    ct,
    len_ref,
    pt_ref,
    parts,
    mate,
    joined,
    moved,
    local_sem,
    send_sem,
    column_sem,
    plane_sem,
    diag_sem,
    pair_sem,
    part_sem,
    mate_sem,
    ready_sem,
    near_sem,
    reach_sem,
):
    me = lax.axis_index("ctx")
    line = n // 8
    core = me % 2
    x = (me // 2) % 2
    y = (me // 4) % 2
    z = me // 8
    far_x, far_y = 1 - x, 1 - y
    rows = lat_hbm.shape[0]
    heads = dq_ref.shape[1]
    chips = n // 2
    chip = me // 2
    span = qt.shape[1]
    cache_dev = ct.shape[2]
    split = rows // 2 if rows % 32 == 0 else rows

    def block(bz, by, bx, bc):
        return ((bz * 2 + by) * 2 + bx) * 2 + bc

    x_peer = block(z, y, far_x, core)
    y_peer = block(z, far_y, x, core)
    pair = block(z, y, x, 1 - core)

    def local(index, source, target):
        copy = pltpu.make_async_copy(source, target, local_sem.at[index])
        copy.start()
        return copy

    own_copy = local(0, lat_hbm, held.at[me])
    c_copy = local(1, ct_hbm, ct)
    d_copy = local(2, dq_hbm, dq_ref)
    len_copy = local(3, len_hbm, len_ref)
    pt_copy = local(4, pt_hbm, pt_ref)
    q_copy = local(5, qt_hbm, qt)

    barrier = pltpu.get_barrier_semaphore()
    peers = ((x, x_peer), (y, y_peer), (core, pair))
    for side, target in peers:

        @pl.when(side == 0)
        def _(target=target):
            pl.semaphore_signal(barrier, inc=1, device_id={"ctx": target})

    def greet(bz, carry):
        pl.semaphore_signal(barrier, inc=1, device_id={"ctx": block(bz, y, x, core)})
        return carry

    lax.fori_loop(z + 1, line, greet, 0)

    @pl.when((z == 0) & (y == 0))
    def _():
        pl.semaphore_signal(barrier, inc=1, device_id={"ctx": block(line - 1, far_y, far_x, core)})

    def both(distance, act):
        if distance == 0:
            act(z)
            return
        pl.when(z + distance < line)(lambda: act(z + distance))
        pl.when(z >= distance)(lambda: act(z - distance))

    def move(index, recv, target, part=None):
        ref = held.at[index]
        if part == 0:
            ref = held.at[index, pl.ds(0, split)]
        if part == 1:
            ref = held.at[index, pl.ds(split, rows - split)]
        pltpu.make_async_remote_copy(
            src_ref=ref, dst_ref=ref, send_sem=send_sem, recv_sem=recv, device_id={"ctx": target}
        ).start()

    def blocks_wait(sem, count):
        ref = held.at[pl.ds(0, count)]
        pltpu.make_async_copy(ref, ref, sem).wait()

    def to_pair(bz, by, bx):
        index = block(bz, by, bx, core)
        move(index, pair_sem.at[bz], pair)

    def spread(bz):
        index = block(bz, y, x, core)
        move(index, plane_sem.at[bz], x_peer)
        move(index, plane_sem.at[bz], y_peer)
        to_pair(bz, y, x)

    def column_step(bz):
        blocks_wait(column_sem.at[bz], 1)
        spread(bz)

    def relay_y(bz):
        if split < rows:
            move(block(bz, y, far_x, core), diag_sem.at[bz], y_peer, 1)

    def relay_x(bz):
        move(block(bz, far_y, x, core), diag_sem.at[bz], x_peer, 0)

    def plane_step(bz, first=False):
        blocks_wait(plane_sem.at[bz], 2)
        if first:
            pl.when(y == 0)(lambda: move(block(bz, y, far_x, core), diag_sem.at[bz], y_peer))
        else:
            relay_y(bz)
            relay_x(bz)
        to_pair(bz, y, far_x)
        to_pair(bz, far_y, x)

    def diag_step(bz):
        blocks_wait(diag_sem.at[bz], 1)
        to_pair(bz, far_y, far_x)

    def up_step(distance):
        @pl.when(z + distance < line)
        def _():
            pl.semaphore_wait(ready_sem.at[z + distance], 1)
            own(column_sem.at[z], block(z + distance, y, x, core))

    def own(recv, target):
        pltpu.make_async_remote_copy(
            src_ref=lat_hbm,
            dst_ref=held.at[me],
            send_sem=send_sem,
            recv_sem=recv,
            device_id={"ctx": target},
        ).start()

    def down(bz, carry):
        own(column_sem.at[z], block(bz, y, x, core))
        return carry

    def ready(bz, carry):
        pl.semaphore_signal(ready_sem.at[z], inc=1, device_id={"ctx": block(bz, y, x, core)})
        return carry

    def reach(target, carry):
        pl.semaphore_signal(reach_sem, inc=1, device_id={"ctx": target * 2 + core})
        return carry

    direct = jnp.where(z == line - 1, y, 0)
    entered = z + direct + x + y + core
    pl.when(entered > 0)(lambda: pl.semaphore_wait(barrier, entered))
    lax.fori_loop(0, z, down, 0)

    @pl.when((z == line - 1) & (y == 1))
    def _():
        own(diag_sem.at[z], block(0, far_y, far_x, core))

    plane_sems = (plane_sem, plane_sem, pair_sem)
    for step, (side, target) in enumerate(peers):

        @pl.when(side == 1)
        def _(target=target, step=step):
            pl.semaphore_signal(near_sem.at[step], inc=1, device_id={"ctx": target})
            own(plane_sems[step].at[z], target)

    lax.fori_loop(0, z, ready, 0)
    for step, (side, target) in enumerate(peers):

        @pl.when(side == 0)
        def _(target=target, step=step):
            pl.semaphore_wait(near_sem.at[step], 1)
            own(plane_sems[step].at[z], target)
            if step == 0:
                pl.semaphore_signal(near_sem.at[0], inc=1, device_id={"ctx": target})

    own_copy.wait()
    c_copy.wait()
    d_copy.wait()
    len_copy.wait()
    pt_copy.wait()
    latent = held[me]
    row_page = (me * rows + lax.broadcasted_iota(jnp.int32, (1, rows), 1)) // PAGE
    first_page = me * rows // PAGE
    request_of = jnp.zeros((1, rows), jnp.int32)
    for p in range(max(1, rows // PAGE)):
        page = first_page + p
        request = (pt_ref[0, page] * POOL + pt_ref[1, page]) % REQ
        request_of = jnp.where(row_page == page, request, request_of)
    positions = me * cache_dev + lax.broadcasted_iota(jnp.int32, (1, cache_dev), 1)
    for r in range(REQ):
        queries = dq_ref[r]
        keys = ct[r]
        scores = jnp.dot(queries, keys, preferred_element_type=jnp.float32) * SCALE
        page_scores = (
            lax.dot_general(queries, latent, NT, preferred_element_type=jnp.float32) * SCALE
        )
        ok = positions < len_ref[r]
        page_ok = request_of == r
        scores = jnp.where(ok, scores, NEG)
        page_scores = jnp.where(page_ok, page_scores, NEG)
        top = jnp.maximum(
            jnp.max(scores, axis=1, keepdims=True), jnp.max(page_scores, axis=1, keepdims=True)
        )
        weights = jnp.where(ok, jnp.exp(scores - top), 0.0)
        page_weights = jnp.where(page_ok, jnp.exp(page_scores - top), 0.0)
        total = jnp.sum(weights, axis=1, keepdims=True) + jnp.sum(
            page_weights, axis=1, keepdims=True
        )
        mixed = lax.dot_general(
            weights.astype(jnp.bfloat16), keys[:D_LAT], NT, preferred_element_type=jnp.float32
        ) + jnp.dot(
            page_weights.astype(jnp.bfloat16),
            latent[:, :D_LAT],
            preferred_element_type=jnp.float32,
        )
        lane = lax.broadcasted_iota(jnp.int32, (heads, 128), 1)
        tail = jnp.where(lane < 64, top, total)
        parts[:, :, :, r * MSG : r * MSG + D_LAT] = mixed.reshape(chips, 2, 1, D_LAT)
        parts[:, :, :, r * MSG + D_LAT : (r + 1) * MSG] = tail.reshape(chips, 2, 1, 128)

    mate_copy = pltpu.make_async_remote_copy(
        src_ref=parts.at[:, 1 - core],
        dst_ref=mate,
        send_sem=mate_sem.at[0],
        recv_sem=mate_sem.at[1],
        device_id={"ctx": pair},
    )
    mate_copy.start()

    @pl.when(x == 1)
    def _():
        pl.semaphore_wait(near_sem.at[0], 1)

    pl.semaphore_signal(near_sem.at[3], inc=1, device_id={"ctx": y_peer})

    def part_copy(target):
        return pltpu.make_async_remote_copy(
            src_ref=joined.at[target],
            dst_ref=moved.at[chip],
            send_sem=part_sem.at[0],
            recv_sem=part_sem.at[1],
            device_id={"ctx": target * 2 + core},
        )

    def send_part(target, carry):
        part_copy(target).start()
        return carry

    def join():
        mate_copy.wait_recv()
        for r in range(REQ):
            mine = parts[:, core, :, r * MSG : (r + 1) * MSG].reshape(chips, MSG)
            other = mate[:, :, r * MSG : (r + 1) * MSG].reshape(chips, MSG)
            top_mine = mine[:, D_LAT : D_LAT + 1]
            top_other = other[:, D_LAT : D_LAT + 1]
            top = jnp.maximum(top_mine, top_other)
            sum_both = mine * jnp.exp(top_mine - top) + other * jnp.exp(top_other - top)
            lane = lax.broadcasted_iota(jnp.int32, (chips, 128), 1)
            tail = jnp.where(lane < 64, top, sum_both[:, D_LAT:])
            joined[:, :, r * MSG : r * MSG + D_LAT] = sum_both[:, :D_LAT].reshape(chips, 1, D_LAT)
            joined[:, :, r * MSG + D_LAT : (r + 1) * MSG] = tail.reshape(chips, 1, 128)
        moved[chip] = joined[chip]

    quarter = span // 4
    group = n // 4

    def attend(i, first, last):
        start, count = i * quarter, (last - first) * quarter
        keys = held[first * group : last * group].reshape(count, held.shape[2])
        scores = lax.dot_general(
            q[start : start + quarter], keys, NT, preferred_element_type=jnp.float32
        )
        if last == i + 1:
            row = start + lax.broadcasted_iota(jnp.int32, (quarter, count), 0)
            col = first * quarter + lax.broadcasted_iota(jnp.int32, (quarter, count), 1)
            scores = jnp.where(col <= row, scores, NEG)
        top = jnp.max(scores, axis=1, keepdims=True)
        weights = jnp.exp((scores - top) * SCALE)
        total = jnp.sum(weights, axis=1, keepdims=True)
        mixed = jnp.dot(
            weights.astype(jnp.bfloat16), keys[:, :D_LAT], preferred_element_type=jnp.float32
        )
        return top, total, mixed

    def finish(i, total, mixed):
        pout_ref[i * quarter : (i + 1) * quarter, :] = (mixed / total).astype(jnp.bfloat16)

    def await_group(p):
        for bz in range(p * (line // 4), (p + 1) * (line // 4)):
            blocks_wait(pair_sem.at[bz], 4)

    def transpose_queries():
        q_copy.wait()
        for start in range(0, span, 128):
            q[start : start + 128, :] = qt[:, start : start + 128].T

    transpose_queries()
    join()
    pl.semaphore_wait(near_sem.at[3], 1)
    lax.fori_loop(0, 4 * z, send_part, 0)
    lax.fori_loop(0, 4 * z, reach, 0)
    for step in range(1, line):
        up_step(step)
    for step in range(1, line):
        both(step, column_step)
        if step == 1:
            plane_step(z)
    both(1, plane_step)
    diag_step(z)
    pl.when(z < line - 1)(lambda: pl.semaphore_wait(reach_sem, 4 * (line - 1 - z)))
    lax.fori_loop(4 * z, chip, send_part, 0)
    lax.fori_loop(chip + 1, chips, send_part, 0)
    for step in range(2, line - 1):
        both(step, plane_step)
    pl.when(z == 0)(lambda: plane_step(line - 1, True))
    pl.when(z == line - 1)(lambda: plane_step(0))
    for step in range(1, line):
        both(step, diag_step)

    for p in range(4):
        await_group(p)
    parts_all = moved.at[pl.ds(0, chips - 1)]
    pltpu.make_async_copy(parts_all, parts_all, part_sem.at[1]).wait()
    for r in range(REQ):
        piece = moved[:, :, r * MSG : (r + 1) * MSG].reshape(chips, MSG)
        best = piece[:, D_LAT : D_LAT + 1]
        mass = piece[:, D_LAT + 64 : D_LAT + 65]
        factor = jnp.exp(best - jnp.max(best, axis=0, keepdims=True))
        own_sum = jnp.sum(mass * factor, axis=0, keepdims=True)
        own_out = jnp.sum(piece[:, :D_LAT] * factor, axis=0, keepdims=True)
        dout_ref[r : r + 1, :] = (own_out / own_sum).astype(jnp.bfloat16)

    for i in range(4):
        _, total, mixed = attend(i, 0, i + 1)
        finish(i, total, mixed)

    blocks_wait(send_sem, n - 2)
    pl.when((z > 0) | (y == 0))(lambda: blocks_wait(send_sem, 1))
    pl.when((z == line - 1) & (y == 1))(lambda: blocks_wait(send_sem, 1))
    mate_copy.wait_send()
    pltpu.make_async_copy(parts_all, parts_all, part_sem.at[0]).wait()


def shards(n, prefill_query, prefill_latent, decode_query, cache, lengths, page_table):
    span, head_here, width = prefill_query.shape
    rows = prefill_latent.shape[0]
    heads = decode_query.shape[1]
    cache_dev = cache.shape[1]
    if head_here != 1 or n % 32 or rows * n != span or span % 512:
        raise ValueError("unexpected sizes")
    line = n // 8
    vmem = pl.BlockSpec(memory_space=pltpu.VMEM)
    anywhere = pl.BlockSpec(memory_space=pl.ANY)
    dma = pltpu.SemaphoreType.DMA
    prefill_out, decode_out = pl.pallas_call(
        functools.partial(kernel, n),
        out_shape=(
            pltpu.VMEM((span, D_LAT), jnp.bfloat16),
            pltpu.VMEM((REQ, D_LAT), jnp.bfloat16),
        ),
        in_specs=[anywhere] * 6,
        out_specs=(vmem, vmem),
        scratch_shapes=[
            pltpu.VMEM((n, rows, width), jnp.bfloat16),
            pltpu.VMEM((REQ, heads, width), jnp.bfloat16),
            pltpu.VMEM((width, span), jnp.bfloat16),
            pltpu.VMEM((span, width), jnp.bfloat16),
            pltpu.VMEM((REQ, width, cache_dev), jnp.bfloat16),
            pltpu.SMEM(lengths.shape, jnp.int32),
            pltpu.SMEM(page_table.shape[::-1], jnp.int32),
            pltpu.VMEM((n // 2, 2, 1, REQ * MSG), jnp.float32),
            pltpu.VMEM((n // 2, 1, REQ * MSG), jnp.float32),
            pltpu.VMEM((n // 2, 1, REQ * MSG), jnp.float32),
            pltpu.VMEM((n // 2, 1, REQ * MSG), jnp.float32),
            dma((6,)),
            dma,
            dma((line,)),
            dma((line,)),
            dma((line,)),
            dma((line,)),
            dma((2,)),
            dma((2,)),
            pltpu.SemaphoreType.REGULAR((line,)),
            pltpu.SemaphoreType.REGULAR((4,)),
            pltpu.SemaphoreType.REGULAR,
        ],
        compiler_params=pltpu.CompilerParams(collective_id=0, has_side_effects=True),
    )(
        prefill_query[:, 0, :].T,
        prefill_latent,
        decode_query,
        jnp.swapaxes(cache, 1, 2),
        lengths,
        page_table.T,
    )
    return prefill_out[:, None, :], decode_out[:, None, :]


def solution(mesh):
    in_specs = (
        P("groups", "ctx", None),
        P(("groups", "ctx"), None),
        P("groups", None, None),
        P("groups", "ctx", None),
        P("groups"),
        P("groups", None),
    )
    out_specs = (P("groups", "ctx", None), P("groups", "ctx", None))
    return jax.shard_map(
        functools.partial(shards, mesh.shape["ctx"]),
        mesh=mesh,
        in_specs=in_specs,
        out_specs=out_specs,
        check_vma=False,
    )
```

time: 26.4 us -> 23.7 us (0.90)
  the two profiles are of different devices: /device:TPU:1 before, /device:TPU:9 now
where the time goes in v1:
time: 23.7 us; the launch traced here: 23.5 us
  Pallas kernels  21.3 us (90%)
  local copies, waits for them, and re-layouts  1.55 us (7%)
  between operations  0.64 us (3%)
    pallas_call x1, Pallas kernels, shards(): pl.pallas_call(functools.partial(kernel, n), out_shape=(pltpu.VMEM((span,...  21.3 us
    unnamed x2, local copies, waits for them, and re-layouts  1.55 us

profile of v1, /device:TPU:9, one launch (start us, length us, event | category | flops | bytes accessed | tf_op | source)
XLA Modules:
  0.0 23.5 jit_solution(15609251939154770433)
XLA Ops:
  0.6 21.3 %shard_map.77 = (bf16[1024,512]{1,0:T(8,128)(2,1)S(1)}, bf16[2,512]{1,0:T(2,128)(2,1)S(1)}) custom-call(bf16[576,1024]{1,0:T(8,128)(2,1)} %bitcast.9, bf16[32,576]{1,0:T(8,128)(2,1)} %lat_hbm.1, bf16[2,32,576]{2,1,0:T(8,128)(2,1)} %dq_hbm.1, bf16[2,576,512]{2,1,0:T(8,128)(2,1)} %bitcast.10, s32[2]{0:T(128)} %len_hbm.1, s32[2,64]{1,0:T(2,128)} %bitcast.11), custom_call_target="tpu_custom_call" | custom-call | tf_op jit(solution)/shard_map/pallas_call | solution.py:395
  22.0 1.0 %copy.10 = bf16[1024,1,512]{2,0,1:T(8,128)(2,1)} copy(bf16[1024,1,512]{2,0,1:T(8,128)(2,1)S(1)} %bitcast.7) | data formatting | bytes 2097152
  22.9 0.6 %copy.11 = bf16[2,1,512]{2,0,1:T(2,128)(2,1)} copy(bf16[2,1,512]{2,0,1:T(2,128)(2,1)S(1)} %bitcast.8) | data formatting | bytes 4096

commit v2 on v1

--- a/solution.py
+++ b/solution.py
@@ -79,11 +79,6 @@
         return copy
 
     own_copy = local(0, lat_hbm, held.at[me])
-    c_copy = local(1, ct_hbm, ct)
-    d_copy = local(2, dq_hbm, dq_ref)
-    len_copy = local(3, len_hbm, len_ref)
-    pt_copy = local(4, pt_hbm, pt_ref)
-    q_copy = local(5, qt_hbm, qt)
 
     barrier = pltpu.get_barrier_semaphore()
     peers = ((x, x_peer), (y, y_peer), (core, pair))
@@ -99,9 +94,6 @@
 
     lax.fori_loop(z + 1, line, greet, 0)
 
-    @pl.when((z == 0) & (y == 0))
-    def _():
-        pl.semaphore_signal(barrier, inc=1, device_id={"ctx": block(line - 1, far_y, far_x, core)})
 
     def both(distance, act):
         if distance == 0:
@@ -128,15 +120,17 @@
         index = block(bz, by, bx, core)
         move(index, pair_sem.at[bz], pair)
 
-    def spread(bz):
+    def spread(bz, straight):
         index = block(bz, y, x, core)
         move(index, plane_sem.at[bz], x_peer)
         move(index, plane_sem.at[bz], y_peer)
+        if straight:
+            move(index, diag_sem.at[bz], block(z, far_y, far_x, core))
         to_pair(bz, y, x)
 
-    def column_step(bz):
+    def column_step(bz, straight):
         blocks_wait(column_sem.at[bz], 1)
-        spread(bz)
+        spread(bz, straight)
 
     def relay_y(bz):
         if split < rows:
@@ -145,11 +139,9 @@
     def relay_x(bz):
         move(block(bz, far_y, x, core), diag_sem.at[bz], x_peer, 0)
 
-    def plane_step(bz, first=False):
+    def plane_step(bz, straight=False):
         blocks_wait(plane_sem.at[bz], 2)
-        if first:
-            pl.when(y == 0)(lambda: move(block(bz, y, far_x, core), diag_sem.at[bz], y_peer))
-        else:
+        if not straight:
             relay_y(bz)
             relay_x(bz)
         to_pair(bz, y, far_x)
@@ -186,14 +178,9 @@
         pl.semaphore_signal(reach_sem, inc=1, device_id={"ctx": target * 2 + core})
         return carry
 
-    direct = jnp.where(z == line - 1, y, 0)
-    entered = z + direct + x + y + core
+    entered = z + x + y + core
     pl.when(entered > 0)(lambda: pl.semaphore_wait(barrier, entered))
     lax.fori_loop(0, z, down, 0)
-
-    @pl.when((z == line - 1) & (y == 1))
-    def _():
-        own(diag_sem.at[z], block(0, far_y, far_x, core))
 
     plane_sems = (plane_sem, plane_sem, pair_sem)
     for step, (side, target) in enumerate(peers):
@@ -204,6 +191,11 @@
             own(plane_sems[step].at[z], target)
 
     lax.fori_loop(0, z, ready, 0)
+    d_copy = local(2, dq_hbm, dq_ref)
+    len_copy = local(3, len_hbm, len_ref)
+    pt_copy = local(4, pt_hbm, pt_ref)
+    c_copy = local(1, ct_hbm, ct)
+    q_copy = local(5, qt_hbm, qt)
     for step, (side, target) in enumerate(peers):
 
         @pl.when(side == 0)
@@ -329,31 +321,50 @@
         for bz in range(p * (line // 4), (p + 1) * (line // 4)):
             blocks_wait(pair_sem.at[bz], 4)
 
+    def up_all(first):
+        for step in range(first, line):
+            up_step(step)
+
     def transpose_queries():
         q_copy.wait()
         for start in range(0, span, 128):
             q[start : start + 128, :] = qt[:, start : start + 128].T
 
+    pl.when(z > 0)(lambda: up_all(1))
     transpose_queries()
+    @pl.when(z == 0)
+    def _():
+        up_step(1)
+        column_step(1, False)
+        plane_step(0)
+        up_step(2)
+
     join()
-    pl.semaphore_wait(near_sem.at[3], 1)
-    lax.fori_loop(0, 4 * z, send_part, 0)
-    lax.fori_loop(0, 4 * z, reach, 0)
+
+    @pl.when(z > 0)
+    def _():
+        pl.semaphore_wait(near_sem.at[3], 1)
+        lax.fori_loop(0, 4 * z, send_part, 0)
+        lax.fori_loop(0, 4 * z, reach, 0)
+
+    pl.when(z == 0)(lambda: pl.semaphore_wait(near_sem.at[3], 1))
+    pl.when(z == 0)(lambda: up_all(3))
     for step in range(1, line):
-        up_step(step)
-    for step in range(1, line):
-        both(step, column_step)
         if step == 1:
-            plane_step(z)
-    both(1, plane_step)
-    diag_step(z)
+            pl.when((z > 0) & (z + 1 < line))(lambda: column_step(z + 1, False))
+            pl.when(z > 0)(lambda: column_step(z - 1, False))
+            pl.when(z > 0)(lambda: plane_step(z))
+        else:
+            both(step, lambda bz: column_step(bz, True))
+    both(1, lambda bz: plane_step(bz, False))
     pl.when(z < line - 1)(lambda: pl.semaphore_wait(reach_sem, 4 * (line - 1 - z)))
     lax.fori_loop(4 * z, chip, send_part, 0)
     lax.fori_loop(chip + 1, chips, send_part, 0)
+    diag_step(z)
     for step in range(2, line - 1):
-        both(step, plane_step)
+        both(step, lambda bz: plane_step(bz, True))
     pl.when(z == 0)(lambda: plane_step(line - 1, True))
-    pl.when(z == line - 1)(lambda: plane_step(0))
+    pl.when(z == line - 1)(lambda: plane_step(0, True))
     for step in range(1, line):
         both(step, diag_step)
 
@@ -375,8 +386,7 @@
         finish(i, total, mixed)
 
     blocks_wait(send_sem, n - 2)
-    pl.when((z > 0) | (y == 0))(lambda: blocks_wait(send_sem, 1))
-    pl.when((z == line - 1) & (y == 1))(lambda: blocks_wait(send_sem, 1))
+    blocks_wait(send_sem, 1)
     mate_copy.wait_send()
     pltpu.make_async_copy(parts_all, parts_all, part_sem.at[0]).wait()
 

time: 23.7 us -> 21.7 us (0.916)
  the two profiles are of different devices: /device:TPU:9 before, /device:TPU:17 now
where the time goes in v2:
time: 21.7 us; the launch traced here: 21.5 us
  Pallas kernels  19.3 us (89%)
  local copies, waits for them, and re-layouts  1.55 us (7%)
  between operations  0.64 us (3%)
    pallas_call x1, Pallas kernels, shards(): pl.pallas_call(functools.partial(kernel, n), out_shape=(pltpu.VMEM((span,...  19.3 us
    unnamed x2, local copies, waits for them, and re-layouts  1.55 us

profile of v2, /device:TPU:17, one launch (start us, length us, event | category | flops | bytes accessed | tf_op | source)
XLA Modules:
  0.0 21.5 jit_solution(1552858064394065263)
XLA Ops:
  0.6 19.3 %shard_map.77 = (bf16[1024,512]{1,0:T(8,128)(2,1)S(1)}, bf16[2,512]{1,0:T(2,128)(2,1)S(1)}) custom-call(bf16[576,1024]{1,0:T(8,128)(2,1)} %bitcast.9, bf16[32,576]{1,0:T(8,128)(2,1)} %lat_hbm.1, bf16[2,32,576]{2,1,0:T(8,128)(2,1)} %dq_hbm.1, bf16[2,576,512]{2,1,0:T(8,128)(2,1)} %bitcast.10, s32[2]{0:T(128)} %len_hbm.1, s32[2,64]{1,0:T(2,128)} %bitcast.11), custom_call_target="tpu_custom_call" | custom-call | tf_op jit(solution)/shard_map/pallas_call | solution.py:405
  20.0 1.0 %copy.10 = bf16[1024,1,512]{2,0,1:T(8,128)(2,1)} copy(bf16[1024,1,512]{2,0,1:T(8,128)(2,1)S(1)} %bitcast.7) | data formatting | bytes 2097152
  20.9 0.6 %copy.11 = bf16[2,1,512]{2,0,1:T(2,128)(2,1)} copy(bf16[2,1,512]{2,0,1:T(2,128)(2,1)S(1)} %bitcast.8) | data formatting | bytes 4096

commit v3 on v2

--- a/solution.py
+++ b/solution.py
@@ -296,25 +296,26 @@
     quarter = span // 4
     group = n // 4
 
-    def attend(i, first, last):
-        start, count = i * quarter, (last - first) * quarter
-        keys = held[first * group : last * group].reshape(count, held.shape[2])
+    def score(i):
+        start, stop = i * quarter, (i + 1) * quarter
+        keys = held[: (i + 1) * group].reshape(stop, held.shape[2])
         scores = lax.dot_general(
-            q[start : start + quarter], keys, NT, preferred_element_type=jnp.float32
-        )
-        if last == i + 1:
-            row = start + lax.broadcasted_iota(jnp.int32, (quarter, count), 0)
-            col = first * quarter + lax.broadcasted_iota(jnp.int32, (quarter, count), 1)
-            scores = jnp.where(col <= row, scores, NEG)
+            q[start:stop], keys, NT, preferred_element_type=jnp.float32
+        )
+        row = lax.broadcasted_iota(jnp.int32, (quarter, quarter), 0)
+        col = lax.broadcasted_iota(jnp.int32, (quarter, quarter), 1)
+        last = jnp.where(col <= row, scores[:, start:], NEG)
+        if i:
+            last = jnp.concatenate([scores[:, :start], last], axis=1)
+        return i, keys, last
+
+    def weigh(i, keys, scores):
         top = jnp.max(scores, axis=1, keepdims=True)
         weights = jnp.exp((scores - top) * SCALE)
         total = jnp.sum(weights, axis=1, keepdims=True)
         mixed = jnp.dot(
             weights.astype(jnp.bfloat16), keys[:, :D_LAT], preferred_element_type=jnp.float32
         )
-        return top, total, mixed
-
-    def finish(i, total, mixed):
         pout_ref[i * quarter : (i + 1) * quarter, :] = (mixed / total).astype(jnp.bfloat16)
 
     def await_group(p):
@@ -381,9 +382,12 @@
         own_out = jnp.sum(piece[:, :D_LAT] * factor, axis=0, keepdims=True)
         dout_ref[r : r + 1, :] = (own_out / own_sum).astype(jnp.bfloat16)
 
-    for i in range(4):
-        _, total, mixed = attend(i, 0, i + 1)
-        finish(i, total, mixed)
+    scored = score(0)
+    for i in range(1, 4):
+        after = score(i)
+        weigh(*scored)
+        scored = after
+    weigh(*scored)
 
     blocks_wait(send_sem, n - 2)
     blocks_wait(send_sem, 1)

time: 21.7 us -> 20.9 us (0.963)
  Pallas kernels: 19.3 us -> 18.5 us
    pallas_call x1, Pallas kernels: 19.3 us -> 18.5 us  [shards(): pl.pallas_call(functools.partial(kernel, n), out_shape=(pltpu.VMEM((span,...]
where the time goes in v3:
time: 20.9 us; the launch traced here: 20.7 us
  Pallas kernels  18.5 us (89%)
  local copies, waits for them, and re-layouts  1.55 us (7%)
  between operations  0.64 us (3%)
    pallas_call x1, Pallas kernels, shards(): pl.pallas_call(functools.partial(kernel, n), out_shape=(pltpu.VMEM((span,...  18.5 us
    unnamed x2, local copies, waits for them, and re-layouts  1.55 us

profile of v3, /device:TPU:17, one launch (start us, length us, event | category | flops | bytes accessed | tf_op | source)
XLA Modules:
  0.0 20.7 jit_solution(13902787094583505753)
XLA Ops:
  0.6 18.5 %shard_map.77 = (bf16[1024,512]{1,0:T(8,128)(2,1)S(1)}, bf16[2,512]{1,0:T(2,128)(2,1)S(1)}) custom-call(bf16[576,1024]{1,0:T(8,128)(2,1)} %bitcast.9, bf16[32,576]{1,0:T(8,128)(2,1)} %lat_hbm.1, bf16[2,32,576]{2,1,0:T(8,128)(2,1)} %dq_hbm.1, bf16[2,576,512]{2,1,0:T(8,128)(2,1)} %bitcast.10, s32[2]{0:T(128)} %len_hbm.1, s32[2,64]{1,0:T(2,128)} %bitcast.11), custom_call_target="tpu_custom_call" | custom-call | tf_op jit(solution)/shard_map/pallas_call | solution.py:409
  19.2 1.0 %copy.10 = bf16[1024,1,512]{2,0,1:T(8,128)(2,1)} copy(bf16[1024,1,512]{2,0,1:T(8,128)(2,1)S(1)} %bitcast.7) | data formatting | bytes 2097152
  20.1 0.6 %copy.11 = bf16[2,1,512]{2,0,1:T(2,128)(2,1)} copy(bf16[2,1,512]{2,0,1:T(2,128)(2,1)S(1)} %bitcast.8) | data formatting | bytes 4096

commit v4 on v3

--- a/solution.py
+++ b/solution.py
@@ -39,6 +39,9 @@
     mate,
     joined,
     moved,
+    acc,
+    tops,
+    sums,
     local_sem,
     send_sem,
     column_sem,
@@ -78,7 +81,7 @@
         copy.start()
         return copy
 
-    own_copy = local(0, lat_hbm, held.at[me])
+    own_copy = local(0, lat_hbm, held.at[chip, core])
 
     barrier = pltpu.get_barrier_semaphore()
     peers = ((x, x_peer), (y, y_peer), (core, pair))
@@ -103,17 +106,17 @@
         pl.when(z >= distance)(lambda: act(z - distance))
 
     def move(index, recv, target, part=None):
-        ref = held.at[index]
+        ref = held.at[index // 2, index % 2]
         if part == 0:
-            ref = held.at[index, pl.ds(0, split)]
+            ref = held.at[index // 2, index % 2, pl.ds(0, split)]
         if part == 1:
-            ref = held.at[index, pl.ds(split, rows - split)]
+            ref = held.at[index // 2, index % 2, pl.ds(split, rows - split)]
         pltpu.make_async_remote_copy(
             src_ref=ref, dst_ref=ref, send_sem=send_sem, recv_sem=recv, device_id={"ctx": target}
         ).start()
 
     def blocks_wait(sem, count):
-        ref = held.at[pl.ds(0, count)]
+        ref = held.at[0, 0] if count == 1 else held.at[pl.ds(0, count // 2)]
         pltpu.make_async_copy(ref, ref, sem).wait()
 
     def to_pair(bz, by, bx):
@@ -160,7 +163,7 @@
     def own(recv, target):
         pltpu.make_async_remote_copy(
             src_ref=lat_hbm,
-            dst_ref=held.at[me],
+            dst_ref=held.at[chip, core],
             send_sem=send_sem,
             recv_sem=recv,
             device_id={"ctx": target},
@@ -210,7 +213,7 @@
     d_copy.wait()
     len_copy.wait()
     pt_copy.wait()
-    latent = held[me]
+    latent = held[chip, core]
     row_page = (me * rows + lax.broadcasted_iota(jnp.int32, (1, rows), 1)) // PAGE
     first_page = me * rows // PAGE
     request_of = jnp.zeros((1, rows), jnp.int32)
@@ -296,27 +299,76 @@
     quarter = span // 4
     group = n // 4
 
-    def score(i):
-        start, stop = i * quarter, (i + 1) * quarter
-        keys = held[: (i + 1) * group].reshape(stop, held.shape[2])
+    def score(i, side=None):
+        pairs, before = (i + 1) * group // 2, i * group // 2 * rows
+        if side is None:
+            keys = held[:pairs].reshape(pairs * 2 * rows, held.shape[3])
+            before = before * 2
+        else:
+            keys = held[:pairs, side].reshape(pairs * rows, held.shape[3])
         scores = lax.dot_general(
-            q[start:stop], keys, NT, preferred_element_type=jnp.float32
-        )
-        row = lax.broadcasted_iota(jnp.int32, (quarter, quarter), 0)
-        col = lax.broadcasted_iota(jnp.int32, (quarter, quarter), 1)
-        last = jnp.where(col <= row, scores[:, start:], NEG)
+            q[i * quarter : (i + 1) * quarter], keys, NT, preferred_element_type=jnp.float32
+        )
+        fresh = keys.shape[0] - before
+        col = lax.broadcasted_iota(jnp.int32, (1, fresh), 1)
+        if side is not None:
+            col = col + (col // rows + side) * rows
+        row = lax.broadcasted_iota(jnp.int32, (quarter, fresh), 0)
+        last = jnp.where(col <= row, scores[:, before:], NEG)
         if i:
-            last = jnp.concatenate([scores[:, :start], last], axis=1)
+            last = jnp.concatenate([scores[:, :before], last], axis=1)
         return i, keys, last
 
-    def weigh(i, keys, scores):
-        top = jnp.max(scores, axis=1, keepdims=True)
-        weights = jnp.exp((scores - top) * SCALE)
-        total = jnp.sum(weights, axis=1, keepdims=True)
+    def wide(value, count):
+        return jnp.concatenate([value] * (count // 128), axis=1)
+
+    def weigh(i, keys, scores, first, last):
+        here = slice(i * quarter, (i + 1) * quarter)
+        top = jnp.broadcast_to(jnp.max(scores, axis=1, keepdims=True), (quarter, 128))
+        if not first:
+            old = tops[here, :]
+            top = jnp.maximum(top, old)
+            fade = jnp.exp((old - top) * SCALE)
+        weights = jnp.exp((scores - wide(top, scores.shape[1])) * SCALE)
+        total = jnp.broadcast_to(jnp.sum(weights, axis=1, keepdims=True), (quarter, 128))
         mixed = jnp.dot(
             weights.astype(jnp.bfloat16), keys[:, :D_LAT], preferred_element_type=jnp.float32
         )
-        pout_ref[i * quarter : (i + 1) * quarter, :] = (mixed / total).astype(jnp.bfloat16)
+        if not first:
+            total = total + sums[here, :] * fade
+            mixed = mixed + acc[here, :] * wide(fade, D_LAT)
+        if last:
+            pout_ref[here, :] = (mixed * wide(1.0 / total, D_LAT)).astype(jnp.bfloat16)
+        else:
+            tops[here, :] = top
+            sums[here, :] = total
+            acc[here, :] = mixed
+
+    def attend(side, first, last):
+        scored = score(0, side)
+        for i in range(1, 4):
+            after = score(i, side)
+            weigh(*scored, first, last)
+            scored = after
+        weigh(*scored, first, last)
+
+    parts_all = moved.at[pl.ds(0, chips - 1)]
+
+    def decode_finish():
+        pltpu.make_async_copy(parts_all, parts_all, part_sem.at[1]).wait()
+        for r in range(REQ):
+            piece = moved[:, :, r * MSG : (r + 1) * MSG].reshape(chips, MSG)
+            best = piece[:, D_LAT : D_LAT + 1]
+            mass = piece[:, D_LAT + 64 : D_LAT + 65]
+            factor = jnp.exp(best - jnp.max(best, axis=0, keepdims=True))
+            own_sum = jnp.sum(mass * factor, axis=0, keepdims=True)
+            own_out = jnp.sum(piece[:, :D_LAT] * factor, axis=0, keepdims=True)
+            dout_ref[r : r + 1, :] = (own_out / own_sum).astype(jnp.bfloat16)
+
+    def send_parts():
+        pl.when(z < line - 1)(lambda: pl.semaphore_wait(reach_sem, 4 * (line - 1 - z)))
+        lax.fori_loop(4 * z, chip, send_part, 0)
+        lax.fori_loop(chip + 1, chips, send_part, 0)
 
     def await_group(p):
         for bz in range(p * (line // 4), (p + 1) * (line // 4)):
@@ -358,9 +410,7 @@
         else:
             both(step, lambda bz: column_step(bz, True))
     both(1, lambda bz: plane_step(bz, False))
-    pl.when(z < line - 1)(lambda: pl.semaphore_wait(reach_sem, 4 * (line - 1 - z)))
-    lax.fori_loop(4 * z, chip, send_part, 0)
-    lax.fori_loop(chip + 1, chips, send_part, 0)
+    pl.when(core == 0)(send_parts)
     diag_step(z)
     for step in range(2, line - 1):
         both(step, lambda bz: plane_step(bz, True))
@@ -369,26 +419,15 @@
     for step in range(1, line):
         both(step, diag_step)
 
+    pl.when(core == 1)(send_parts)
+    pl.when(core == 1)(lambda: attend(1, True, False))
+    pl.when(core == 1)(decode_finish)
     for p in range(4):
         await_group(p)
-    parts_all = moved.at[pl.ds(0, chips - 1)]
-    pltpu.make_async_copy(parts_all, parts_all, part_sem.at[1]).wait()
-    for r in range(REQ):
-        piece = moved[:, :, r * MSG : (r + 1) * MSG].reshape(chips, MSG)
-        best = piece[:, D_LAT : D_LAT + 1]
-        mass = piece[:, D_LAT + 64 : D_LAT + 65]
-        factor = jnp.exp(best - jnp.max(best, axis=0, keepdims=True))
-        own_sum = jnp.sum(mass * factor, axis=0, keepdims=True)
-        own_out = jnp.sum(piece[:, :D_LAT] * factor, axis=0, keepdims=True)
-        dout_ref[r : r + 1, :] = (own_out / own_sum).astype(jnp.bfloat16)
-
-    scored = score(0)
-    for i in range(1, 4):
-        after = score(i)
-        weigh(*scored)
-        scored = after
-    weigh(*scored)
-
+    pl.when(core == 0)(lambda: attend(None, True, True))
+    pl.when(core == 1)(lambda: attend(0, False, True))
+
+    pl.when(core == 0)(decode_finish)
     blocks_wait(send_sem, n - 2)
     blocks_wait(send_sem, 1)
     mate_copy.wait_send()
@@ -415,7 +454,7 @@
         in_specs=[anywhere] * 6,
         out_specs=(vmem, vmem),
         scratch_shapes=[
-            pltpu.VMEM((n, rows, width), jnp.bfloat16),
+            pltpu.VMEM((n // 2, 2, rows, width), jnp.bfloat16),
             pltpu.VMEM((REQ, heads, width), jnp.bfloat16),
             pltpu.VMEM((width, span), jnp.bfloat16),
             pltpu.VMEM((span, width), jnp.bfloat16),
@@ -426,6 +465,9 @@
             pltpu.VMEM((n // 2, 1, REQ * MSG), jnp.float32),
             pltpu.VMEM((n // 2, 1, REQ * MSG), jnp.float32),
             pltpu.VMEM((n // 2, 1, REQ * MSG), jnp.float32),
+            pltpu.VMEM((span, D_LAT), jnp.float32),
+            pltpu.VMEM((span, 128), jnp.float32),
+            pltpu.VMEM((span, 128), jnp.float32),
             dma((6,)),
             dma,
             dma((line,)),

time: 20.9 us -> 20 us (0.957)
  Pallas kernels: 18.5 us -> 17.7 us
    pallas_call x1, Pallas kernels: 18.5 us -> 17.7 us  [shards(): pl.pallas_call(functools.partial(kernel, n), out_shape=(pltpu.VMEM((span,...]
where the time goes in v4:
time: 20 us; the launch traced here: 19.9 us
  Pallas kernels  17.7 us (88%)
  local copies, waits for them, and re-layouts  1.55 us (8%)
  between operations  0.64 us (3%)
    pallas_call x1, Pallas kernels, shards(): pl.pallas_call(functools.partial(kernel, n), out_shape=(pltpu.VMEM((span,...  17.7 us
    unnamed x2, local copies, waits for them, and re-layouts  1.55 us

profile of v4, /device:TPU:17, one launch (start us, length us, event | category | flops | bytes accessed | tf_op | source)
XLA Modules:
  0.0 19.9 jit_solution(17939440863666884953)
XLA Ops:
  0.6 17.7 %shard_map.77 = (bf16[1024,512]{1,0:T(8,128)(2,1)S(1)}, bf16[2,512]{1,0:T(2,128)(2,1)S(1)}) custom-call(bf16[576,1024]{1,0:T(8,128)(2,1)} %bitcast.9, bf16[32,576]{1,0:T(8,128)(2,1)} %lat_hbm.1, bf16[2,32,576]{2,1,0:T(8,128)(2,1)} %dq_hbm.1, bf16[2,576,512]{2,1,0:T(8,128)(2,1)} %bitcast.10, s32[2]{0:T(128)} %len_hbm.1, s32[2,64]{1,0:T(2,128)} %bitcast.11), custom_call_target="tpu_custom_call" | custom-call | tf_op jit(solution)/shard_map/pallas_call | solution.py:448
  18.3 1.0 %copy.10 = bf16[1024,1,512]{2,0,1:T(8,128)(2,1)} copy(bf16[1024,1,512]{2,0,1:T(8,128)(2,1)S(1)} %bitcast.7) | data formatting | bytes 2097152
  19.3 0.6 %copy.11 = bf16[2,1,512]{2,0,1:T(2,128)(2,1)} copy(bf16[2,1,512]{2,0,1:T(2,128)(2,1)S(1)} %bitcast.8) | data formatting | bytes 4096

commit v5 on v4

--- a/solution.py
+++ b/solution.py
@@ -432,6 +432,17 @@
     blocks_wait(send_sem, 1)
     mate_copy.wait_send()
     pltpu.make_async_copy(parts_all, parts_all, part_sem.at[0]).wait()
+
+
+def store(prefill_ref, decode_ref, prefill_hbm, decode_hbm, sem):
+    copies = (
+        pltpu.make_async_copy(decode_ref, decode_hbm, sem.at[0]),
+        pltpu.make_async_copy(prefill_ref, prefill_hbm, sem.at[1]),
+    )
+    for copy in copies:
+        copy.start()
+    for copy in copies:
+        copy.wait()
 
 
 def shards(n, prefill_query, prefill_latent, decode_query, cache, lengths, page_table):
@@ -489,6 +500,16 @@
         lengths,
         page_table.T,
     )
+    prefill_out, decode_out = pl.pallas_call(
+        store,
+        out_shape=(
+            jax.ShapeDtypeStruct((span, D_LAT), jnp.bfloat16),
+            jax.ShapeDtypeStruct((REQ, D_LAT), jnp.bfloat16),
+        ),
+        in_specs=[vmem, vmem],
+        out_specs=(anywhere, anywhere),
+        scratch_shapes=[dma((2,))],
+    )(*(pltpu.with_memory_space_constraint(a, pltpu.VMEM) for a in (prefill_out, decode_out)))
     return prefill_out[:, None, :], decode_out[:, None, :]
 
 

time: 20 us -> 19.5 us (0.975)
  local copies, waits for them, and re-layouts: 1.55 us -> 0 us
  Pallas kernels: 17.7 us -> 18.7 us
    unnamed x2 -> x0, local copies, waits for them, and re-layouts: 1.55 us -> none
    pallas_call x0 -> x1, Pallas kernels: none -> 0.99 us  [shards(): pl.pallas_call(store, out_shape=(jax.ShapeDtypeStruct((span, D_LAT), jnp....]
where the time goes in v5:
time: 19.5 us; the launch traced here: 19.3 us
  Pallas kernels  18.7 us (96%)
  between operations  0.64 us (3%)
    pallas_call x1, Pallas kernels, shards(): pl.pallas_call(functools.partial(kernel, n), out_shape=(pltpu.VMEM((span,...  17.7 us
    pallas_call x1, Pallas kernels, shards(): pl.pallas_call(store, out_shape=(jax.ShapeDtypeStruct((span, D_LAT), jnp....  0.99 us

profile of v5, /device:TPU:17, one launch (start us, length us, event | category | flops | bytes accessed | tf_op | source)
XLA Modules:
  0.0 19.3 jit_solution(14731664136020814174)
XLA Ops:
  0.6 17.7 %shard_map.77 = (bf16[1024,512]{1,0:T(8,128)(2,1)S(1)}, bf16[2,512]{1,0:T(2,128)(2,1)S(1)}) custom-call(bf16[576,1024]{1,0:T(8,128)(2,1)} %bitcast.7, bf16[32,576]{1,0:T(8,128)(2,1)} %lat_hbm.1, bf16[2,32,576]{2,1,0:T(8,128)(2,1)} %dq_hbm.1, bf16[2,576,512]{2,1,0:T(8,128)(2,1)} %bitcast.8, s32[2]{0:T(128)} %len_hbm.1, s32[2,64]{1,0:T(2,128)} %bitcast.9), custom_call_target="tpu_custom_call" | custom-call | tf_op jit(solution)/shard_map/pallas_call | solution.py:459
  18.3 1.0 %shard_map.78 = (bf16[1024,512]{1,0:T(8,128)(2,1)}, bf16[2,512]{1,0:T(2,128)(2,1)}) custom-call(bf16[1024,512]{1,0:T(8,128)(2,1)S(1)} %get-tuple-element.6.prefill_ref, bf16[2,512]{1,0:T(2,128)(2,1)S(1)} %get-tuple-element.7.decode_ref), custom_call_target="tpu_custom_call" | custom-call | tf_op jit(solution)/shard_map/pallas_call | solution.py:503

commit v6 on v4

--- a/solution.py
+++ b/solution.py
@@ -14,8 +14,71 @@
 
 SCALE = 192.0 ** (-0.5)
 NEG = -1e30
+VMEM_LIMIT = 56 * 2**20
 MSG = D_LAT + 128
 NT = (((1,), (1,)), ((), ()))
+
+
+def score(refs, i, side):
+    held, q, acc, tops, sums = refs
+    rows = held.shape[2]
+    quarter, group = q.shape[0] // 4, held.shape[0] // 2
+    pairs, before = (i + 1) * group // 2, i * group // 2 * rows
+    if side is None:
+        keys = held[:pairs].reshape(pairs * 2 * rows, held.shape[3])
+        before = before * 2
+    else:
+        keys = held[:pairs, side].reshape(pairs * rows, held.shape[3])
+    scores = lax.dot_general(
+        q[i * quarter : (i + 1) * quarter], keys, NT, preferred_element_type=jnp.float32
+    )
+    fresh = keys.shape[0] - before
+    col = lax.broadcasted_iota(jnp.int32, (1, fresh), 1)
+    if side is not None:
+        col = col + (col // rows + side) * rows
+    row = lax.broadcasted_iota(jnp.int32, (quarter, fresh), 0)
+    last = jnp.where(col <= row, scores[:, before:], NEG)
+    if i:
+        last = jnp.concatenate([scores[:, :before], last], axis=1)
+    return i, keys, last
+
+
+def wide(value, count):
+    return jnp.concatenate([value] * (count // 128), axis=1)
+
+
+def weigh(refs, i, keys, scores, first, emit):
+    held, q, acc, tops, sums = refs
+    quarter = q.shape[0] // 4
+    here = slice(i * quarter, (i + 1) * quarter)
+    top = jnp.broadcast_to(jnp.max(scores, axis=1, keepdims=True), (quarter, 128))
+    if not first:
+        old = tops[here, :]
+        top = jnp.maximum(top, old)
+        fade = jnp.exp((old - top) * SCALE)
+    weights = jnp.exp((scores - wide(top, scores.shape[1])) * SCALE)
+    total = jnp.broadcast_to(jnp.sum(weights, axis=1, keepdims=True), (quarter, 128))
+    mixed = jnp.dot(
+        weights.astype(jnp.bfloat16), keys[:, :D_LAT], preferred_element_type=jnp.float32
+    )
+    if not first:
+        total = total + sums[here, :] * fade
+        mixed = mixed + acc[here, :] * wide(fade, D_LAT)
+    if emit is not None:
+        emit(i, (mixed * wide(1.0 / total, D_LAT)).astype(jnp.bfloat16))
+    else:
+        tops[here, :] = top
+        sums[here, :] = total
+        acc[here, :] = mixed
+
+
+def attend(refs, side, first, emit):
+    scored = score(refs, 0, side)
+    for i in range(1, 4):
+        after = score(refs, i, side)
+        weigh(refs, *scored, first, emit)
+        scored = after
+    weigh(refs, *scored, first, emit)
 
 
 def kernel(
@@ -26,12 +89,15 @@
     ct_hbm,
     len_hbm,
     pt_hbm,
+    held,
+    q,
+    acc,
+    tops,
+    sums,
     pout_ref,
     dout_ref,
-    held,
     dq_ref,
     qt,
-    q,
     ct,
     len_ref,
     pt_ref,
@@ -39,9 +105,6 @@
     mate,
     joined,
     moved,
-    acc,
-    tops,
-    sums,
     local_sem,
     send_sem,
     column_sem,
@@ -102,8 +165,8 @@
         if distance == 0:
             act(z)
             return
+        pl.when(z >= distance)(lambda: act(z - distance))
         pl.when(z + distance < line)(lambda: act(z + distance))
-        pl.when(z >= distance)(lambda: act(z - distance))
 
     def move(index, recv, target, part=None):
         ref = held.at[index // 2, index % 2]
@@ -299,59 +362,6 @@
     quarter = span // 4
     group = n // 4
 
-    def score(i, side=None):
-        pairs, before = (i + 1) * group // 2, i * group // 2 * rows
-        if side is None:
-            keys = held[:pairs].reshape(pairs * 2 * rows, held.shape[3])
-            before = before * 2
-        else:
-            keys = held[:pairs, side].reshape(pairs * rows, held.shape[3])
-        scores = lax.dot_general(
-            q[i * quarter : (i + 1) * quarter], keys, NT, preferred_element_type=jnp.float32
-        )
-        fresh = keys.shape[0] - before
-        col = lax.broadcasted_iota(jnp.int32, (1, fresh), 1)
-        if side is not None:
-            col = col + (col // rows + side) * rows
-        row = lax.broadcasted_iota(jnp.int32, (quarter, fresh), 0)
-        last = jnp.where(col <= row, scores[:, before:], NEG)
-        if i:
-            last = jnp.concatenate([scores[:, :before], last], axis=1)
-        return i, keys, last
-
-    def wide(value, count):
-        return jnp.concatenate([value] * (count // 128), axis=1)
-
-    def weigh(i, keys, scores, first, last):
-        here = slice(i * quarter, (i + 1) * quarter)
-        top = jnp.broadcast_to(jnp.max(scores, axis=1, keepdims=True), (quarter, 128))
-        if not first:
-            old = tops[here, :]
-            top = jnp.maximum(top, old)
-            fade = jnp.exp((old - top) * SCALE)
-        weights = jnp.exp((scores - wide(top, scores.shape[1])) * SCALE)
-        total = jnp.broadcast_to(jnp.sum(weights, axis=1, keepdims=True), (quarter, 128))
-        mixed = jnp.dot(
-            weights.astype(jnp.bfloat16), keys[:, :D_LAT], preferred_element_type=jnp.float32
-        )
-        if not first:
-            total = total + sums[here, :] * fade
-            mixed = mixed + acc[here, :] * wide(fade, D_LAT)
-        if last:
-            pout_ref[here, :] = (mixed * wide(1.0 / total, D_LAT)).astype(jnp.bfloat16)
-        else:
-            tops[here, :] = top
-            sums[here, :] = total
-            acc[here, :] = mixed
-
-    def attend(side, first, last):
-        scored = score(0, side)
-        for i in range(1, 4):
-            after = score(i, side)
-            weigh(*scored, first, last)
-            scored = after
-        weigh(*scored, first, last)
-
     parts_all = moved.at[pl.ds(0, chips - 1)]
 
     def decode_finish():
@@ -404,8 +414,8 @@
     pl.when(z == 0)(lambda: up_all(3))
     for step in range(1, line):
         if step == 1:
+            pl.when(z > 0)(lambda: column_step(z - 1, False))
             pl.when((z > 0) & (z + 1 < line))(lambda: column_step(z + 1, False))
-            pl.when(z > 0)(lambda: column_step(z - 1, False))
             pl.when(z > 0)(lambda: plane_step(z))
         else:
             both(step, lambda bz: column_step(bz, True))
@@ -420,18 +430,53 @@
         both(step, diag_step)
 
     pl.when(core == 1)(send_parts)
-    pl.when(core == 1)(lambda: attend(1, True, False))
+    refs = (held, q, acc, tops, sums)
+    pl.when(core == 1)(lambda: attend(refs, 1, True, None))
     pl.when(core == 1)(decode_finish)
     for p in range(4):
         await_group(p)
-    pl.when(core == 0)(lambda: attend(None, True, True))
-    pl.when(core == 1)(lambda: attend(0, False, True))
-
+
+
+    def emit(i, value):
+        pout_ref[i * quarter : (i + 1) * quarter, :] = value
+
+    pl.when(core == 0)(lambda: attend(refs, None, True, emit))
     pl.when(core == 0)(decode_finish)
     blocks_wait(send_sem, n - 2)
     blocks_wait(send_sem, 1)
     mate_copy.wait_send()
     pltpu.make_async_copy(parts_all, parts_all, part_sem.at[0]).wait()
+
+
+def store(
+    held, q, acc, tops, sums, whole_ref, decode_ref, prefill_hbm, decode_hbm, rows_ref, sem
+):
+    quarter = q.shape[0] // 4
+    core = lax.axis_index("ctx") % 2
+    decode_copy = pltpu.make_async_copy(decode_ref, decode_hbm, sem.at[4])
+    decode_copy.start()
+
+    def chunk_copy(i):
+        here = pl.ds(i * quarter, quarter)
+        return pltpu.make_async_copy(rows_ref.at[here], prefill_hbm.at[here], sem.at[i])
+
+    def emit(i, value):
+        rows_ref[i * quarter : (i + 1) * quarter, :] = value
+        chunk_copy(i).start()
+
+    @pl.when(core == 0)
+    def _():
+        copy = pltpu.make_async_copy(whole_ref, prefill_hbm, sem.at[0])
+        copy.start()
+        copy.wait()
+
+    @pl.when(core == 1)
+    def _():
+        attend((held, q, acc, tops, sums), 0, False, emit)
+        for i in range(4):
+            chunk_copy(i).wait()
+
+    decode_copy.wait()
 
 
 def shards(n, prefill_query, prefill_latent, decode_query, cache, lengths, page_table):
@@ -445,19 +490,22 @@
     vmem = pl.BlockSpec(memory_space=pltpu.VMEM)
     anywhere = pl.BlockSpec(memory_space=pl.ANY)
     dma = pltpu.SemaphoreType.DMA
-    prefill_out, decode_out = pl.pallas_call(
+    state = pl.pallas_call(
         functools.partial(kernel, n),
         out_shape=(
+            pltpu.VMEM((n // 2, 2, rows, width), jnp.bfloat16),
+            pltpu.VMEM((span, width), jnp.bfloat16),
+            pltpu.VMEM((span, D_LAT), jnp.float32),
+            pltpu.VMEM((span, 128), jnp.float32),
+            pltpu.VMEM((span, 128), jnp.float32),
             pltpu.VMEM((span, D_LAT), jnp.bfloat16),
             pltpu.VMEM((REQ, D_LAT), jnp.bfloat16),
         ),
         in_specs=[anywhere] * 6,
-        out_specs=(vmem, vmem),
+        out_specs=(vmem,) * 7,
         scratch_shapes=[
-            pltpu.VMEM((n // 2, 2, rows, width), jnp.bfloat16),
             pltpu.VMEM((REQ, heads, width), jnp.bfloat16),
             pltpu.VMEM((width, span), jnp.bfloat16),
-            pltpu.VMEM((span, width), jnp.bfloat16),
             pltpu.VMEM((REQ, width, cache_dev), jnp.bfloat16),
             pltpu.SMEM(lengths.shape, jnp.int32),
             pltpu.SMEM(page_table.shape[::-1], jnp.int32),
@@ -465,9 +513,6 @@
             pltpu.VMEM((n // 2, 1, REQ * MSG), jnp.float32),
             pltpu.VMEM((n // 2, 1, REQ * MSG), jnp.float32),
             pltpu.VMEM((n // 2, 1, REQ * MSG), jnp.float32),
-            pltpu.VMEM((span, D_LAT), jnp.float32),
-            pltpu.VMEM((span, 128), jnp.float32),
-            pltpu.VMEM((span, 128), jnp.float32),
             dma((6,)),
             dma,
             dma((line,)),
@@ -480,7 +525,9 @@
             pltpu.SemaphoreType.REGULAR((4,)),
             pltpu.SemaphoreType.REGULAR,
         ],
-        compiler_params=pltpu.CompilerParams(collective_id=0, has_side_effects=True),
+        compiler_params=pltpu.CompilerParams(
+            collective_id=0, has_side_effects=True, vmem_limit_bytes=VMEM_LIMIT
+        ),
     )(
         prefill_query[:, 0, :].T,
         prefill_latent,
@@ -489,6 +536,17 @@
         lengths,
         page_table.T,
     )
+    prefill_out, decode_out = pl.pallas_call(
+        store,
+        out_shape=(
+            jax.ShapeDtypeStruct((span, D_LAT), jnp.bfloat16),
+            jax.ShapeDtypeStruct((REQ, D_LAT), jnp.bfloat16),
+        ),
+        in_specs=[vmem] * 7,
+        out_specs=(anywhere, anywhere),
+        scratch_shapes=[pltpu.VMEM((span, D_LAT), jnp.bfloat16), dma((5,))],
+        compiler_params=pltpu.CompilerParams(vmem_limit_bytes=VMEM_LIMIT),
+    )(*(pltpu.with_memory_space_constraint(a, pltpu.VMEM) for a in state))
     return prefill_out[:, None, :], decode_out[:, None, :]
 
 

time: 20 us -> 19.2 us (0.960)
  local copies, waits for them, and re-layouts: 1.55 us -> 0 us
  Pallas kernels: 17.7 us -> 18.3 us
    unnamed x2 -> x0, local copies, waits for them, and re-layouts: 1.55 us -> none
    pallas_call x1 -> x2, Pallas kernels: 17.7 us -> 18.3 us  [the longest x1 15.9 us: shards(): pl.pallas_call(functools.partial(kernel, n), out_shape=(pltpu.VMEM((n //...]
where the time goes in v6:
time: 19.2 us; the launch traced here: 19 us
  Pallas kernels  18.3 us (95%)
  between operations  0.64 us (3%)
    pallas_call x1, Pallas kernels, shards(): pl.pallas_call(functools.partial(kernel, n), out_shape=(pltpu.VMEM((n //...  15.9 us
    pallas_call x1, Pallas kernels, shards(): pl.pallas_call(store, out_shape=(jax.ShapeDtypeStruct((span, D_LAT), jnp....  2.38 us

profile of v6, /device:TPU:17, one launch (start us, length us, event | category | flops | bytes accessed | tf_op | source)
XLA Modules:
  0.0 19.0 jit_solution(10149817584236847343)
XLA Ops:
  0.6 15.9 %shard_map.77 = (bf16[16,2,32,576]{3,2,1,0:T(8,128)(2,1)S(1)}, bf16[1024,576]{1,0:T(8,128)(2,1)S(1)}, f32[1024,512]{1,0:T(8,128)S(1)}, f32[1024,128]{1,0:T(8,128...) custom-call(bf16[576,1024]{1,0:T(8,128)(2,1)} %bitcast.7, ...), custom_call_target="tpu_custom_call" | custom-call | tf_op jit(solution)/shard_map/pallas_call | solution.py:493
  16.6 2.4 %shard_map.78 = (bf16[1024,512]{1,0:T(8,128)(2,1)}, bf16[2,512]{1,0:T(2,128)(2,1)}) custom-call(bf16[16,2,32,576]{3,2,1,0:T(8,128)(2,1)S(1)} %get-tuple-element.11.held, bf16[1024,576]{1,0:T(8,128)(2,1)S(1)} %get-tuple-element.12.q, f32[1024,512]{1,0:T(8,128)S(1)} %get-tuple-element.13.acc, f32[1024,128]{1,0:T(8,128)S(1)} %get-tuple-element.14.tops, ...), custom_call_target="tpu_custom_call" | custom-call | tf_op jit(solution)/shard_map/pallas_call | solution.py:539

commit v7 on v6

--- a/solution.py
+++ b/solution.py
@@ -73,8 +73,8 @@
 
 
 def attend(refs, side, first, emit):
-    scored = score(refs, 0, side)
-    for i in range(1, 4):
+    scored = score(refs, 3, side)
+    for i in (2, 1, 0):
         after = score(refs, i, side)
         weigh(refs, *scored, first, emit)
         scored = after
@@ -186,12 +186,17 @@
         index = block(bz, by, bx, core)
         move(index, pair_sem.at[bz], pair)
 
+    def choose(condition, act):
+        if condition is True:
+            act()
+        elif condition is not False:
+            pl.when(condition)(act)
+
     def spread(bz, straight):
         index = block(bz, y, x, core)
         move(index, plane_sem.at[bz], x_peer)
         move(index, plane_sem.at[bz], y_peer)
-        if straight:
-            move(index, diag_sem.at[bz], block(z, far_y, far_x, core))
+        choose(straight, lambda: move(index, diag_sem.at[bz], block(z, far_y, far_x, core)))
         to_pair(bz, y, x)
 
     def column_step(bz, straight):
@@ -207,9 +212,12 @@
 
     def plane_step(bz, straight=False):
         blocks_wait(plane_sem.at[bz], 2)
-        if not straight:
+
+        def relay():
             relay_y(bz)
             relay_x(bz)
+
+        choose(not straight if isinstance(straight, bool) else core == 1, relay)
         to_pair(bz, y, far_x)
         to_pair(bz, far_y, x)
 
@@ -418,12 +426,12 @@
             pl.when((z > 0) & (z + 1 < line))(lambda: column_step(z + 1, False))
             pl.when(z > 0)(lambda: plane_step(z))
         else:
-            both(step, lambda bz: column_step(bz, True))
+            both(step, lambda bz, far=(core == 0) if step <= 2 else True: column_step(bz, far))
     both(1, lambda bz: plane_step(bz, False))
     pl.when(core == 0)(send_parts)
     diag_step(z)
     for step in range(2, line - 1):
-        both(step, lambda bz: plane_step(bz, True))
+        both(step, lambda bz, far=(core == 0) if step <= 2 else True: plane_step(bz, far))
     pl.when(z == 0)(lambda: plane_step(line - 1, True))
     pl.when(z == line - 1)(lambda: plane_step(0, True))
     for step in range(1, line):

time: 19.2 us -> 19.1 us (level)
  no operation moved by 1% of the time
where the time goes in v7:
time: 19.1 us; the launch traced here: 19 us
  Pallas kernels  18.3 us (96%)
  between operations  0.64 us (3%)
    pallas_call x1, Pallas kernels, shards(): pl.pallas_call(functools.partial(kernel, n), out_shape=(pltpu.VMEM((n //...  15.9 us
    pallas_call x1, Pallas kernels, shards(): pl.pallas_call(store, out_shape=(jax.ShapeDtypeStruct((span, D_LAT), jnp....  2.38 us

profile of v7, /device:TPU:17, one launch (start us, length us, event | category | flops | bytes accessed | tf_op | source)
XLA Modules:
  0.0 19.0 jit_solution(5906476244648360477)
XLA Ops:
  0.6 15.9 %shard_map.77 = (bf16[16,2,32,576]{3,2,1,0:T(8,128)(2,1)S(1)}, bf16[1024,576]{1,0:T(8,128)(2,1)S(1)}, f32[1024,512]{1,0:T(8,128)S(1)}, f32[1024,128]{1,0:T(8,128...) custom-call(bf16[576,1024]{1,0:T(8,128)(2,1)} %bitcast.7, ...), custom_call_target="tpu_custom_call" | custom-call | tf_op jit(solution)/shard_map/pallas_call | solution.py:501
  16.6 2.4 %shard_map.78 = (bf16[1024,512]{1,0:T(8,128)(2,1)}, bf16[2,512]{1,0:T(2,128)(2,1)}) custom-call(bf16[16,2,32,576]{3,2,1,0:T(8,128)(2,1)S(1)} %get-tuple-element.11.held, bf16[1024,576]{1,0:T(8,128)(2,1)S(1)} %get-tuple-element.12.q, f32[1024,512]{1,0:T(8,128)S(1)} %get-tuple-element.13.acc, f32[1024,128]{1,0:T(8,128)S(1)} %get-tuple-element.14.tops, ...), custom_call_target="tpu_custom_call" | custom-call | tf_op jit(solution)/shard_map/pallas_call | solution.py:547
